TPU v7x, 32 devices: a whole 2x2x4 slice. The times are simulated.
32 devices in a mesh: ao: 8 (over y, x, core), aux: 4 (over z).
Axes of the slice: x: 2, y: 2, z: 4, core: 2. Of those that a mesh axis runs over, the one named last changes fastest.
Arguments:
- blocks: bfloat16 [48, 256, 128, 128], P('ao', 'aux'), may hold values from -6 to 6
- pairs: int32 [48, 2], P('ao'), may hold values from 0 to 79, as said below
- counts: int32 [8], P('ao'), may hold values from 1 to 6, as said below
- owned_blocks: int32 [80], P('ao'), may hold values from 0 to 79, as said below
- occ_coef: bfloat16 [80, 8, 128], P('ao'), may hold values from -0.5 to 0.5
- vir_coef: bfloat16 [10240, 9216], P('ao', 'aux'), may hold values from -0.109375 to 0.109375
Outputs:
- b_tensor: bfloat16 [256, 8, 9216], P('ao', None, 'aux')
Inputs may be any that keep to these rules, and one draw needn't show every extreme that they name: `pairs`: among the used slots of one ao index, at most 3 have nu blocks whose rows one owner holds; in every draw some index reaches 3. `counts`: some ao index uses all 6 slots in every draw. `owned_blocks`: every atom block appears exactly once.
All inputs are finite; a program needn't handle non-finite values.
Results may differ from a plain program's by a relative error of at most 0.014.
Values may be sent and summed in bfloat16 or wider, within the bound.
A program may use at most 128 MiB of HBM per device.

v0:
```python
import jax
import jax.numpy as jnp
from jax import lax
from jax.sharding import PartitionSpec as P


def block_place(block_ids, owned_all):
    hits = block_ids[..., None] == owned_all
    positions = jnp.arange(owned_all.shape[0], dtype=jnp.int32)
    return jnp.sum(jnp.where(hits, positions, 0), axis=-1)


def per_device(blocks, pairs, counts, owned_blocks, occ_coef, vir_coef):
    groups = lax.axis_size("ao")
    own_index = lax.axis_index("ao")
    slot_count = blocks.shape[0]
    aux_depth = blocks.shape[1]
    block_width = blocks.shape[3]
    occupied = occ_coef.shape[1]
    all_pairs, all_counts, all_owned = (
        lax.all_gather(pairs, "ao", axis=0, tiled=True),
        lax.all_gather(counts, "ao", axis=0, tiled=True),
        lax.all_gather(owned_blocks, "ao", axis=0, tiled=True),
    )
    occ_all = lax.all_gather(occ_coef, "ao", axis=0, tiled=True)
    total_blocks = all_owned.shape[0]
    per_owner = total_blocks // groups
    slot_ids = jnp.arange(slot_count, dtype=jnp.int32)
    in_use = slot_ids < counts[0]
    occ_pick = occ_all[block_place(pairs[:, 0], all_owned)]
    slab_values = jnp.einsum("sim,spmn->spin", occ_pick, blocks, preferred_element_type=jnp.float32)
    slab_values = jnp.where(in_use[:, None, None, None], slab_values, 0.0).astype(jnp.bfloat16)
    flat_slabs = slab_values.reshape(slot_count, aux_depth * occupied, block_width)
    place_all = block_place(all_pairs[:, 1], all_owned).reshape(groups, slot_count)
    owner_all = place_all // per_owner
    local_all = place_all % per_owner
    live_all = slot_ids[None, :] < all_counts[:, None]
    mine_all = live_all & (owner_all == own_index)
    local_ids = jnp.arange(per_owner, dtype=jnp.int32)
    slabs_got = lax.all_gather(flat_slabs, "ao", axis=0, tiled=True)
    assign = (
        mine_all.reshape(-1)[None, :] & (local_all.reshape(-1)[None, :] == local_ids[:, None])
    ).astype(jnp.bfloat16)
    summed = jnp.einsum("lt,tqm->qlm", assign, slabs_got, preferred_element_type=jnp.float32)
    rows_local = summed.reshape(summed.shape[0], per_owner * block_width).astype(jnp.bfloat16)
    rows_whole = lax.all_gather(rows_local, "aux", axis=0, tiled=True)
    share = rows_whole.shape[0] // groups
    result = lax.psum_scatter(
        jnp.dot(rows_whole, vir_coef, preferred_element_type=jnp.float32).astype(jnp.bfloat16),
        "ao",
        scatter_dimension=0,
        tiled=True,
    ).astype(jnp.float32)
    return result.reshape(share // occupied, occupied, vir_coef.shape[1]).astype(jnp.bfloat16)


def solution(mesh):
    in_specs = (
        P("ao", "aux", None, None),
        P("ao", None),
        P("ao"),
        P("ao"),
        P("ao", None, None),
        P("ao", "aux"),
    )
    out_specs = P("ao", None, "aux")
    return jax.shard_map(
        per_device, mesh=mesh, in_specs=in_specs, out_specs=out_specs, check_vma=False
    )
```

profile of v0, /device:TPU:0, one launch (start us, length us, event | category | flops | bytes accessed | tf_op | source)
XLA Modules:
  0.0 291.0 jit_solution(9892513670469097050)
XLA Ops:
  6.5 0.0 all-gather.4.cloned.1.call-start
  7.2 0.7 slice_bitcast_fusion.1
  7.9 1.3 dynamic-slice
  9.9 0.8 dynamic-update-slice.1
  10.7 0.8 dynamic-update-slice
  11.5 9.5 %all-reduce.2 = (s32[80]{0:T(128)S(1)}, s32[8]{0:T(128)S(1)}) all-reduce(s32[80]{0:T(128)S(1)} %dynamic-update-slice, s32[8]{0:T(128)S(1)} %dynamic-update-slice.1), channel_id=1, replica_groups=mesh['ao'=8,'aux'=4] {'ao'}, use_global_device_ids=true, to_apply=%add | all-reduce | flops 88 | bytes 704
  21.0 0.2 select_reduce_fusion.1
  21.2 8.6 %all_gather.18 = bf16[80,8,128]{2,1,0:T(8,128)(2,1)S(1)} all-gather(bf16[10,8,128]{2,1,0:T(8,128)(2,1)} %param.10), channel_id=1, replica_groups=mesh['ao'=8,'aux'=4] {'ao'}, dimensions={0}, use_global_device_ids=true | all-gather | bytes 184320 | tf_op jit(solution)/shard_map/all_gather | solution.py:25
  29.8 0.6 gather_fusion
  30.4 0.0 copy-start
  30.4 7.2 %fusion.4 = bf16[6,512,128]{2,1,0:T(8,128)(2,1)} fusion(bf16[6,64,128,128]{3,2,1,0:T(8,128)(2,1)} %param.6, pred[6]{0:T(512)(128)(4,1)S(1)} %iota_compare_fusion.2, bf16[6,8,128]{2,1,0:T(8,128)(2,1)S(1)} %gather_fusion), kind=kOutput, calls=%fused_computation.6 | convolution fusion | flops 101449728 | bytes 13381638 | tf_op jit(solution)/shard_map/sim,spmn->spin/dot_general | solution.py:31
  37.6 0.0 all-gather.4.cloned.1.call-update
  37.6 0.0 all-gather.6.cloned.1.call-start
  37.7 0.1 iota_compare_fusion.1
  37.8 0.1 lt.52
  37.9 0.0 copy-done
  37.9 8.6 %all-gather = s32[8,6,2]{1,2,0:T(2,128)S(1)} all-gather(s32[1,6,2]{1,2,0:T(2,128)S(1)} %bitcast.35), channel_id=1, replica_groups=mesh['ao'=8,'aux'=4] {'ao'}, dimensions={0}, use_global_device_ids=true | all-gather | bytes 432 | tf_op jit(solution)/shard_map/all_gather | solution.py:21
  46.5 0.1 reshape.75
  46.5 0.2 select_reduce_fusion
  46.8 36.7 %all-gather.4.cloned.1.call-done = bf16[48,512,128]{2,1,0:T(8,128)(2,1)} async-done(((bf16[6,512,128]{2,1,0:T(8,128)(2,1)}), bf16[48,512,128]{2,1,0:T(8,128)(2,1)}) %all-gather.4.cloned.1.call-update) | async-done | bytes 6291472 | tf_op jit(solution)/shard_map/all_gather | solution.py:40
  83.5 6.4 %convert_bitcast_fusion = bf16[512,10,128]{2,1,0:T(8,128)(2,1)S(1)} fusion(bf16[48,512,128]{2,1,0:T(8,128)(2,1)} %all-gather.4.cloned.1.call-done, s32[48]{0:T(128)S(1)} %and_select_fusion, pred[48]{0:T(512)(128)(4,1)S(1)} %compare_and_fusion), kind=kOutput, calls=%fused_computation.4 | convolution fusion | flops 63570880 | bytes 7602416 | tf_op jit(solution)/shard_map/lt,tqm->qlm/dot_general | solution.py:44
  89.9 2.6 copy.17
  92.5 0.0 all-gather.6.cloned.1.call-update
  92.5 0.2 reduce-scatter.2.cloned.1.call-start
  92.7 98.0 %all-gather.6.cloned.1.call-done = bf16[2048,1280]{0,1:T(8,128)(2,1)} async-done(((bf16[512,1280]{0,1:T(8,128)(2,1)}), bf16[2048,1280]{0,1:T(8,128)(2,1)}) %all-gather.6.cloned.1.call-update) | async-done | bytes 5242896 | tf_op jit(solution)/shard_map/all_gather | solution.py:46
  190.7 18.4 %convolution_convert_fusion = bf16[2048,2304]{1,0:T(8,128)(2,1)} fusion(bf16[2048,1280]{0,1:T(8,128)(2,1)} %all-gather.6.cloned.1.call-done, bf16[1280,2304]{1,0:T(8,128)(2,1)} %param.11), kind=kOutput, calls=%fused_computation.1 | convolution fusion | flops 12084314112 | bytes 20578304 | tf_op jit(solution)/shard_map/dot_general | solution.py:49
  209.1 0.0 reduce-scatter.2.cloned.1.call-update
  209.1 75.3 %reduce-scatter.2.cloned.1.call-done = bf16[256,2304]{1,0:T(8,128)(2,1)} async-done(((bf16[2048,2304]{1,0:T(8,128)(2,1)}), bf16[256,2304]{1,0:T(8,128)(2,1)}) %reduce-scatter.2.cloned.1.call-update) | async-done | bytes 1179664 | tf_op jit(solution)/shard_map/reduce_scatter | solution.py:48
  (9 shorter events, 0.1 us)
Async XLA Ops:
  6.5 76.9 %all-gather.4.cloned.1.call-start = ((), (), s32[]{:S(2)}) async-start(), calls=%async_computation.1 | async-start | bytes 7077888 | tf_op jit(solution)/shard_map/all_gather | solution.py:40
  30.4 7.5 %copy-start = (s32[6,2]{0,1:T(2,128)S(1)}, s32[6,2]{0,1:T(2,128)}, u32[]{:S(2)}) copy-start(s32[6,2]{0,1:T(2,128)} %param.7) | copy-start | bytes 148
  37.6 153.0 %all-gather.6.cloned.1.call-start = ((), (), s32[]{:S(2)}) async-start(), calls=%async_computation.2 | async-start | bytes 6553600 | tf_op jit(solution)/shard_map/all_gather | solution.py:46
  92.5 191.9 %reduce-scatter.2.cloned.1.call-start = ((), (), s32[]{:S(2)}) async-start(), calls=%async_computation.3 | async-start | bytes 10616832 | tf_op jit(solution)/shard_map/reduce_scatter | solution.py:48
Sparse Core Ops, SparseCore 0:
  37.8 45.6 all-gather.3
  92.6 98.0 all-gather.5
  209.2 75.1 reduce-scatter.1
where the time goes:
time: 291 us
  waiting for transfers between devices  210 us (72%)
  matrix products  32.1 us (11%)
  blocking collectives  26.7 us (9%)
  between operations  14.5 us (5%)
  local copies, waits for them, and re-layouts  6.95 us (2%)
    all_gather x1, waiting for transfers between devices, per_device(): rows_whole = lax.all_gather(rows_local, 'aux', axis=0, tiled=True)  98 us
    reduce_scatter x1, waiting for transfers between devices, per_device(): lax.psum_scatter(jnp.dot(rows_whole, vir_coef, preferred_element_type=jnp...  75.3 us
    all_gather x1, waiting for transfers between devices, per_device(): slabs_got = lax.all_gather(flat_slabs, 'ao', axis=0, tiled=True)  36.7 us
    dot_general x1, matrix products, per_device(): jnp.dot(rows_whole, vir_coef, preferred_element_type=jnp.float32)  18.4 us
    unnamed x1, blocking collectives  9.49 us
    all_gather x1, blocking collectives, per_device(): occ_all = lax.all_gather(occ_coef, 'ao', axis=0, tiled=True)  8.6 us
    all_gather x1, blocking collectives, per_device(): lax.all_gather(pairs, 'ao', axis=0, tiled=True)  8.59 us
    dot_general x1, matrix products, per_device(): jnp.einsum('sim,spmn->spin', occ_pick, blocks, preferred_element_type=jnp...  7.2 us
  transfers between devices with their start and end apart: 3, of which 3 were waited for; matrix products, arithmetic and copies ran while one was open for 0% of the time, Pallas kernels for 0%

commit v1 on v0

--- a/solution.py
+++ b/solution.py
@@ -2,6 +2,40 @@
 import jax.numpy as jnp
 from jax import lax
 from jax.sharding import PartitionSpec as P
+
+
+def search_the_core(incoming_x, row_dim):
+    mesh_ax = "aux"
+    new, clean, newest = (
+        lax.axis_size(mesh_ax),
+        lax.axis_index(mesh_ax),
+        incoming_x.shape[row_dim],
+    )
+    f_now = lax.dynamic_update_slice_in_dim(
+        jnp.zeros(
+            [at * new if s == row_dim else at for s, at in enumerate(incoming_x.shape)],
+            incoming_x.dtype,
+        ),
+        incoming_x,
+        clean * newest,
+        axis=row_dim,
+    )
+    t_next = then = incoming_x
+    for dev_j in range(1, new // 2 + 1):
+        t_next = lax.ppermute(
+            t_next, axis_name=mesh_ax, perm=[(s, (s + 1) % new) for s in range(new)]
+        )
+        f_now = lax.dynamic_update_slice_in_dim(
+            f_now, t_next, (clean - dev_j) % new * newest, axis=row_dim
+        )
+        if 2 * dev_j < new:
+            then = lax.ppermute(
+                then, axis_name=mesh_ax, perm=[(s, (s - 1) % new) for s in range(new)]
+            )
+            f_now = lax.dynamic_update_slice_in_dim(
+                f_now, then, (clean + dev_j) % new * newest, axis=row_dim
+            )
+    return f_now
 
 
 def block_place(block_ids, owned_all):
@@ -43,7 +77,7 @@
     ).astype(jnp.bfloat16)
     summed = jnp.einsum("lt,tqm->qlm", assign, slabs_got, preferred_element_type=jnp.float32)
     rows_local = summed.reshape(summed.shape[0], per_owner * block_width).astype(jnp.bfloat16)
-    rows_whole = lax.all_gather(rows_local, "aux", axis=0, tiled=True)
+    rows_whole = search_the_core(rows_local, 0)
     share = rows_whole.shape[0] // groups
     result = lax.psum_scatter(
         jnp.dot(rows_whole, vir_coef, preferred_element_type=jnp.float32).astype(jnp.bfloat16),

time: 291 us -> 279 us (0.959)
  waiting for transfers between devices: 210 us -> 195 us
  starting transfers between devices: 0.27 us -> 3.92 us
  matrix products: 32.1 us -> 28.9 us
    all_gather x1 -> x0, waiting for transfers between devices: 98 us -> none  [per_device(): rows_whole = lax.all_gather(rows_local, 'aux', axis=0, tiled=True)]
    ppermute x0 -> x3, waiting for transfers between devices: none -> 82.7 us  [the longest x2 56.8 us: search_the_core(): lax.ppermute(t_next, axis_name=mesh_ax, perm=[(s, (s + 1) % new) for s in...]
    ppermute x0 -> x3, starting transfers between devices: none -> 3.88 us  [the longest x1 2.34 us: search_the_core(): lax.ppermute(then, axis_name=mesh_ax, perm=[(s, (s - 1) % new) for s in r...]
    dynamic_update_slice x0 -> x4, local copies, waits for them, and re-layouts: none -> 3.35 us  [the longest x2 1.68 us: search_the_core(): lax.dynamic_update_slice_in_dim(f_now, t_next, (clean - dev_j) % new * ne...]
    dot_general x1, matrix products: 18.4 us -> 15.2 us  [per_device(): jnp.dot(rows_whole, vir_coef, preferred_element_type=jnp.float32)]
  transfers between devices with their start and end apart: 3 -> 5, of which waited for: 3 -> 5; matrix products, arithmetic and copies ran while one was open for 0% -> 1% of each run, Pallas kernels for 0% -> 0%
where the time goes in v1:
time: 279 us
  waiting for transfers between devices  195 us (70%)
  matrix products  28.9 us (10%)
  blocking collectives  26.7 us (10%)
  between operations  14.8 us (5%)
  local copies, waits for them, and re-layouts  9.78 us (4%)
  starting transfers between devices  3.92 us (1%)
    reduce_scatter x1, waiting for transfers between devices, per_device(): lax.psum_scatter(jnp.dot(rows_whole, vir_coef, preferred_element_type=jnp...  75.1 us
    ppermute x2, waiting for transfers between devices, search_the_core(): lax.ppermute(t_next, axis_name=mesh_ax, perm=[(s, (s + 1) % new) for s in...  56.8 us
    all_gather x1, waiting for transfers between devices, per_device(): slabs_got = lax.all_gather(flat_slabs, 'ao', axis=0, tiled=True)  36.7 us
    ppermute x1, waiting for transfers between devices, search_the_core(): lax.ppermute(then, axis_name=mesh_ax, perm=[(s, (s - 1) % new) for s in r...  25.9 us
    dot_general x1, matrix products, per_device(): jnp.dot(rows_whole, vir_coef, preferred_element_type=jnp.float32)  15.2 us
    unnamed x1, blocking collectives  9.49 us
    all_gather x1, blocking collectives, per_device(): occ_all = lax.all_gather(occ_coef, 'ao', axis=0, tiled=True)  8.6 us
    all_gather x1, blocking collectives, per_device(): lax.all_gather(pairs, 'ao', axis=0, tiled=True)  8.6 us
  transfers between devices with their start and end apart: 5, of which 5 were waited for; matrix products, arithmetic and copies ran while one was open for 1% of the time, Pallas kernels for 0%

profile of v1, /device:TPU:0, one launch (start us, length us, event | category | flops | bytes accessed | tf_op | source)
XLA Modules:
  0.0 279.1 jit_solution(15695172732687264339)
XLA Ops:
  6.5 0.0 all-gather.3.cloned.1.call-start
  7.2 0.7 slice_bitcast_fusion.1
  7.9 1.3 dynamic-slice
  9.8 0.7 dynamic-update-slice.1
  10.5 0.8 dynamic-update-slice
  11.3 9.5 %all-reduce.2 = (s32[80]{0:T(128)S(1)}, s32[8]{0:T(128)S(1)}) all-reduce(s32[80]{0:T(128)S(1)} %dynamic-update-slice, s32[8]{0:T(128)S(1)} %dynamic-update-slice.1), channel_id=1, replica_groups=mesh['ao'=8,'aux'=4] {'ao'}, use_global_device_ids=true, to_apply=%add | all-reduce | flops 88 | bytes 704
  20.8 0.2 select_reduce_fusion.1
  21.0 8.6 %all_gather.15 = bf16[80,8,128]{2,1,0:T(8,128)(2,1)S(1)} all-gather(bf16[10,8,128]{2,1,0:T(8,128)(2,1)} %param.10), channel_id=1, replica_groups=mesh['ao'=8,'aux'=4] {'ao'}, dimensions={0}, use_global_device_ids=true | all-gather | bytes 184320 | tf_op jit(solution)/shard_map/all_gather | solution.py:59
  29.6 0.6 gather_fusion
  30.2 0.0 copy-start
  30.2 7.2 %fusion.4 = bf16[6,512,128]{2,1,0:T(8,128)(2,1)} fusion(bf16[6,64,128,128]{3,2,1,0:T(8,128)(2,1)} %param.6, pred[6]{0:T(512)(128)(4,1)S(1)} %iota_compare_fusion.2, bf16[6,8,128]{2,1,0:T(8,128)(2,1)S(1)} %gather_fusion), kind=kOutput, calls=%fused_computation.6 | convolution fusion | flops 101449728 | bytes 13381638 | tf_op jit(solution)/shard_map/sim,spmn->spin/dot_general | solution.py:65
  37.4 0.0 all-gather.3.cloned.1.call-update
  37.4 0.0 reduce-scatter.2.cloned.1.call-start
  37.5 0.0 copy-done
  37.5 8.6 %all-gather = s32[8,6,2]{1,2,0:T(2,128)S(1)} all-gather(s32[1,6,2]{1,2,0:T(2,128)S(1)} %bitcast.37), channel_id=1, replica_groups=mesh['ao'=8,'aux'=4] {'ao'}, dimensions={0}, use_global_device_ids=true | all-gather | bytes 432 | tf_op jit(solution)/shard_map/all_gather | solution.py:55
  46.1 0.1 reshape.75
  46.2 0.1 iota_compare_fusion.1
  46.2 0.1 lt.78
  46.3 0.2 select_reduce_fusion
  46.6 36.7 %all-gather.3.cloned.1.call-done = bf16[48,512,128]{2,1,0:T(8,128)(2,1)} async-done(((bf16[6,512,128]{2,1,0:T(8,128)(2,1)}), bf16[48,512,128]{2,1,0:T(8,128)(2,1)}) %all-gather.3.cloned.1.call-update) | async-done | bytes 6291472 | tf_op jit(solution)/shard_map/all_gather | solution.py:74
  83.2 6.4 %convert_bitcast_fusion = bf16[512,10,128]{2,1,0:T(8,128)(2,1)S(1)} fusion(bf16[48,512,128]{2,1,0:T(8,128)(2,1)} %all-gather.3.cloned.1.call-done, s32[48]{0:T(128)S(1)} %and_select_fusion, pred[48]{0:T(512)(128)(4,1)S(1)} %compare_and_fusion), kind=kOutput, calls=%fused_computation.4 | convolution fusion | flops 63570880 | bytes 7602416 | tf_op jit(solution)/shard_map/lt,tqm->qlm/dot_general | solution.py:78
  89.7 1.5 copy.17
  91.2 1.5 collective-permute-start
  92.7 2.3 collective-permute-start.1
  95.1 29.7 %collective-permute-done = bf16[512,1280]{0,1:T(8,128)(2,1)S(1)} collective-permute-done((bf16[512,1280]{0,1:T(8,128)(2,1)S(1)}, bf16[512,1280]{0,1:T(8,128)(2,1)S(1)}, u32[]{:S(2)}, u32[]{:S(2)}) %collective-permute-start) | collective-permute-done | bytes 1310752 | tf_op jit(solution)/shard_map/ppermute | solution.py:25
  124.8 0.0 collective-permute-start.2
  124.8 0.0 slice-start
  124.8 0.6 broadcast_in_dim.38
  125.4 0.2 constant_dynamic-update-slice_fusion.3
  125.6 0.0 slice-start.1
  125.6 0.2 constant_dynamic-update-slice_fusion.2
  125.8 25.9 %collective-permute-done.1 = bf16[512,1280]{0,1:T(8,128)(2,1)} collective-permute-done((bf16[512,1280]{0,1:T(8,128)(2,1)S(1)}, bf16[512,1280]{0,1:T(8,128)(2,1)}, u32[]{:S(2)}, u32[]{:S(2)}) %collective-permute-start.1) | collective-permute-done | bytes 1310752 | tf_op jit(solution)/shard_map/ppermute | solution.py:32
  151.7 1.5 constant_dynamic-update-slice_fusion.1
  153.2 27.1 %collective-permute-done.2 = bf16[512,1280]{0,1:T(8,128)(2,1)} collective-permute-done((bf16[512,1280]{0,1:T(8,128)(2,1)S(1)}, bf16[512,1280]{0,1:T(8,128)(2,1)}, u32[]{:S(2)}, u32[]{:S(2)}) %collective-permute-start.2) | collective-permute-done | bytes 1310752 | tf_op jit(solution)/shard_map/ppermute | solution.py:25
  180.3 1.5 constant_dynamic-update-slice_fusion
  181.8 0.0 slice-done
  181.8 0.0 slice-done.1
  181.8 15.2 %convolution_convert_fusion = bf16[2048,2304]{1,0:T(8,128)(2,1)} fusion(bf16[2048,1280]{0,1:T(8,128)(2,1)S(1)} %constant_dynamic-update-slice_fusion, bf16[1280,2304]{1,0:T(8,128)(2,1)S(1)} %bitcast.39), kind=kOutput, calls=%fused_computation.1 | convolution fusion | flops 12084314112 | bytes 20578304 | tf_op jit(solution)/shard_map/dot_general | solution.py:83
  197.1 0.0 reduce-scatter.2.cloned.1.call-update
  197.1 75.1 %reduce-scatter.2.cloned.1.call-done = bf16[256,2304]{1,0:T(8,128)(2,1)} async-done(((bf16[2048,2304]{1,0:T(8,128)(2,1)}), bf16[256,2304]{1,0:T(8,128)(2,1)}) %reduce-scatter.2.cloned.1.call-update) | async-done | bytes 1179664 | tf_op jit(solution)/shard_map/reduce_scatter | solution.py:82
  (10 shorter events, 0.1 us)
Async XLA Ops:
  6.5 76.7 %all-gather.3.cloned.1.call-start = ((), (), s32[]{:S(2)}) async-start(), calls=%async_computation.1 | async-start | bytes 7077888 | tf_op jit(solution)/shard_map/all_gather | solution.py:74
  30.2 7.3 %copy-start = (s32[6,2]{0,1:T(2,128)S(1)}, s32[6,2]{0,1:T(2,128)}, u32[]{:S(2)}) copy-start(s32[6,2]{0,1:T(2,128)} %param.7) | copy-start | bytes 148
  37.4 234.8 %reduce-scatter.2.cloned.1.call-start = ((), (), s32[]{:S(2)}) async-start(), calls=%async_computation.2 | async-start | bytes 10616832 | tf_op jit(solution)/shard_map/reduce_scatter | solution.py:82
  91.2 33.5 %collective-permute-start = (bf16[512,1280]{0,1:T(8,128)(2,1)S(1)}, bf16[512,1280]{0,1:T(8,128)(2,1)S(1)}, u32[]{:S(2)}, u32[]{:S(2)}) collective-permute-start(bf16[512,1280]{0,1:T(8,128)(2,1)S(1)} %bitcast.34), channel_id=1, source_target_pairs={{0,1},{1,2},{2,3},{3,0},{4,5},{5,6},{6,7},{7,4},{8,9},{9,10},{10,1... | collective-permute-start | bytes 3932168 | tf_op jit(solution)/shard_map/ppermute | solution.py:25
  92.7 58.9 %collective-permute-start.1 = (bf16[512,1280]{0,1:T(8,128)(2,1)S(1)}, bf16[512,1280]{0,1:T(8,128)(2,1)}, u32[]{:S(2)}, u32[]{:S(2)}) collective-permute-start(bf16[512,1280]{0,1:T(8,128)(2,1)S(1)} %bitcast.35), channel_id=1, source_target_pairs={{0,3},{1,0},{2,1},{3,2},{4,7},{5,4},{6,5},{7,6},{8,11},{9,8},{10,9... | collective-permute-start | bytes 3932168 | tf_op jit(solution)/shard_map/ppermute | solution.py:32
  124.8 55.6 %collective-permute-start.2 = (bf16[512,1280]{0,1:T(8,128)(2,1)S(1)}, bf16[512,1280]{0,1:T(8,128)(2,1)}, u32[]{:S(2)}, u32[]{:S(2)}) collective-permute-start(bf16[512,1280]{0,1:T(8,128)(2,1)S(1)} %collective-permute-done), channel_id=1, source_target_pairs={{0,1},{1,2},{2,3},{3,0},{4,5},{5,6},{6,7},{7,4},{8,9},{9,10},{10,1... | collective-permute-start | bytes 3932168 | tf_op jit(solution)/shard_map/ppermute | solution.py:25
  124.8 57.1 %slice-start = ((s8[5898240]{0:T(1024)(128)(4,1)}), s8[4194304]{0:T(1024)(128)(4,1)S(1)}, s32[]{:S(2)}) async-start(s8[5898240]{0:T(1024)(128)(4,1)} %bitcast.38), calls=%async_computation.3 | async-start | bytes 8388608
  125.6 56.2 %slice-start.1 = ((s8[5898240]{0:T(1024)(128)(4,1)}), s8[1703936]{0:T(1024)(128)(4,1)S(1)}, s32[]{:S(2)}) async-start(s8[5898240]{0:T(1024)(128)(4,1)} %bitcast.38), calls=%async_computation.4 | async-start | bytes 3407872
Sparse Core Ops, SparseCore 0:
  37.5 45.6 all-gather.2
  197.2 74.9 reduce-scatter.1
